TPU v7x, 256 devices: a whole 4x4x8 slice. The times are simulated.
256 devices in a mesh: dp: 8 (over y_hi, x), blk: 32 (over z, y_lo, core).
Axes of the slice: x: 4, y: 4 (y_hi: 2, y_lo: 2; y = y_hi * 2 + y_lo), z: 8, core: 2. Of those that a mesh axis runs over, the one named last changes fastest.
Arguments:
- particles: float32 [4096, 1024], P('blk'), may hold values from -14 to 14
- data_rows: bfloat16 [32768, 1024], P('dp'), may hold values from -0.1875 to 0.1875
- labels: int32 [32768], P('dp'), may hold values from 0 to 1
Outputs:
- descent: float32 [4096, 1024], P('blk')
All inputs are finite; a program needn't handle non-finite values.
Results may differ from a plain program's by a relative error of at most 0.0045.
Values may be sent and summed in bfloat16 or wider, within the bound.
A program may use at most 64 MiB of HBM per device.

v0:
```python
import jax
import jax.numpy as jnp
from jax import lax
from jax.sharding import Mesh
from jax.sharding import PartitionSpec as P

BLK = ("blk_0", "blk_1", "blk_2")


prior_var = 4.0


def from_everyone(value, axis):
    devices = lax.axis_size(axis)
    return lax.all_to_all(
        jnp.broadcast_to(value[None], (devices, *value.shape)), axis, 0, 0, tiled=True
    )


def over_copies(value, axis):
    everything = from_everyone(value, axis)
    return jnp.sum(everything.astype(jnp.float32), axis=0)


def joined_along(blocks, dim):
    blocks = jnp.moveaxis(blocks, 0, dim)
    shape = blocks.shape
    return blocks.reshape(*shape[:dim], shape[dim] * shape[dim + 1], *shape[dim + 2 :])


def whole_of(value, axes, dim):
    far, near = axes
    blocks = from_everyone(from_everyone(value, far), near)
    return joined_along(blocks.swapaxes(0, 1).reshape(-1, *value.shape), dim)


def sent_together(arrays, axis, dim, along):
    widths = [a.shape[along] for a in arrays]
    both = jnp.concatenate(arrays, axis=along)
    whole = whole_of(both, axis, dim)
    return tuple(jnp.split(whole, [sum(widths[:k]) for k in range(1, len(widths))], axis=along))


def pair_sums(left_x, left_s, right_x, right_s, inv_band):
    feature_count = left_x.shape[1]
    left_xf = left_x.astype(jnp.float32)
    left_sf = left_s.astype(jnp.float32)
    right_xf = right_x.astype(jnp.float32)
    right_sf = right_s.astype(jnp.float32)
    left_norm = jnp.sum(left_xf * left_xf, axis=1)
    right_norm = jnp.sum(right_xf * right_xf, axis=1)
    left_sx = jnp.sum(left_sf * left_xf, axis=1)
    right_sx = jnp.sum(right_sf * right_xf, axis=1)
    gram_xx = jnp.einsum("id,jd->ij", left_x, right_x, preferred_element_type=jnp.float32)
    gram_ss = jnp.einsum("id,jd->ij", left_s, right_s, preferred_element_type=jnp.float32)
    cross_dot = jnp.einsum(
        "id,jd->ij",
        jnp.concatenate([left_x, left_s], axis=1),
        jnp.concatenate([right_s, right_x], axis=1),
        preferred_element_type=jnp.float32,
    )
    distance = left_norm[:, None] + right_norm[None, :] - 2.0 * gram_xx
    kernel = jnp.exp(-0.5 * inv_band * distance)
    bracket = (
        gram_ss
        + inv_band * (left_sx[:, None] - cross_dot + right_sx[None, :])
        + feature_count * inv_band
        - inv_band * inv_band * distance
    )
    weighted_kernel = kernel * bracket
    kernel_sum = jnp.sum(kernel, axis=1)
    weighted_sum = jnp.sum(weighted_kernel, axis=1)
    both_rows = jnp.dot(
        kernel.astype(jnp.bfloat16),
        jnp.concatenate([right_x, right_s], axis=1),
        preferred_element_type=jnp.float32,
    )
    kernel_x = both_rows[:, :feature_count]
    kernel_s = both_rows[:, feature_count:]
    weighted_x = jnp.dot(
        weighted_kernel.astype(jnp.bfloat16), right_x, preferred_element_type=jnp.float32
    )
    return (kernel_sum, weighted_sum, kernel_x, kernel_s, weighted_x)


def forces(left_x, left_s, sums, inv_band, particle_count):
    kernel_sum, weighted_sum, kernel_x, kernel_s, weighted_x = sums
    left_xf = left_x.astype(jnp.float32)
    left_sf = left_s.astype(jnp.float32)
    spread = kernel_sum[:, None] * left_xf - kernel_x
    score_force = (kernel_s + inv_band * spread) / particle_count
    place_force = (
        -inv_band * (weighted_sum[:, None] * left_xf - weighted_x)
        + inv_band * (kernel_sum[:, None] * left_sf - kernel_s)
        - 2.0 * inv_band * inv_band * spread
    ) / particle_count
    return (score_force, place_force)


def empty_sums(rows_count, feature_count):
    flat_zero = jnp.zeros((rows_count,), jnp.float32)
    wide_zero = jnp.zeros((rows_count, feature_count), jnp.float32)
    return (flat_zero, flat_zero, wide_zero, wide_zero, wide_zero)


def pair_folder(left_x, left_s, inv_band, running, pieces):
    pair_parts = pair_sums(left_x, left_s, pieces[0], pieces[1], inv_band)
    return jax.tree.map(jnp.add, running, pair_parts)


def shards(particles, data_rows, labels):
    block_rows, feature_count = particles.shape
    groups_count = lax.axis_size("dp")
    particle_count = block_rows * lax.axis_size(BLK)
    inv_band = 1.0 / feature_count
    x_low = particles.astype(jnp.bfloat16)
    logits = jnp.einsum("pd,md->pm", x_low, data_rows, preferred_element_type=jnp.float32)
    probability = jax.nn.sigmoid(logits)
    residual = (labels.astype(jnp.float32)[None, :] - probability).astype(jnp.bfloat16)
    curvature = probability * (1.0 - probability)
    partial_score = jnp.dot(residual, data_rows, preferred_element_type=jnp.float32)
    scores = (
        over_copies(partial_score.astype(jnp.bfloat16), "dp").astype(jnp.float32)
        - particles / prior_var
    )
    s_low = scores.astype(jnp.bfloat16)
    share_rows = block_rows // groups_count
    offset = lax.axis_index("dp") * share_rows
    right_x = lax.dynamic_slice_in_dim(x_low, offset, share_rows, 0)
    right_s = lax.dynamic_slice_in_dim(s_low, offset, share_rows, 0)
    sums = pair_folder(
        x_low,
        s_low,
        inv_band,
        empty_sums(block_rows, feature_count),
        sent_together((right_x, right_s), (("blk_0", "blk_1"), "blk_2"), 0, 1),
    )
    score_force, own_place = forces(x_low, s_low, sums, inv_band, particle_count)
    full_force = over_copies(score_force.astype(jnp.bfloat16), "dp").astype(jnp.float32)
    projected = jnp.einsum(
        "pd,md->pm", full_force.astype(jnp.bfloat16), data_rows, preferred_element_type=jnp.float32
    )
    weighted_rows = (curvature * projected).astype(jnp.bfloat16)
    data_term = jnp.dot(weighted_rows, data_rows, preferred_element_type=jnp.float32)
    summed = over_copies((data_term - own_place).astype(jnp.bfloat16), "dp").astype(jnp.float32)
    return summed + full_force / prior_var


def solution(mesh):
    torus = Mesh(mesh.devices.reshape(mesh.shape["dp"], 8, 2, 2), ("dp", "blk_0", "blk_1", "blk_2"))
    return jax.shard_map(
        shards,
        mesh=torus,
        in_specs=(P(BLK, None), P("dp", None), P("dp")),
        out_specs=P(BLK, None),
        check_vma=False,
    )
```

profile of v0, /device:TPU:1, one launch (start us, length us, event | category | flops | bytes accessed | tf_op | source)
XLA Modules:
  0.0 179.0 jit_solution(2277040423226146729)
XLA Ops:
  0.0 1.2 convert_element_type.56
  1.2 0.9 convert_element_type.58
  2.1 6.5 %fusion.3 = f32[128,4096]{1,0:T(8,128)S(1)} fusion(bf16[128,1024]{1,0:T(8,128)(2,1)S(1)} %convert_element_type.56, bf16[4096,1024]{1,0:T(8,128)(2,1)} %param.4), kind=kOutput, calls=%fused_computation.5 | convolution fusion | flops 1075314688 | bytes 10747904 | tf_op jit(solution)/shard_map/pd,md->pm/dot_general | solution.py:117
  8.7 1.3 convolution_convert_fusion
  10.0 1.6 broadcast_in_dim.10
  11.6 7.5 %all-to-all-start = ((bf16[8,128,1024]{2,1,0:T(8,128)(2,1)}), bf16[8,128,1024]{2,1,0:T(8,128)(2,1)S(1)}, u32[]{:S(2)}, u32[]{:S(2)}) async-start(bf16[8,128,1024]{2,1,0:T(8,128)(2,1)} %broadcast_in_dim.10), calls=%async_computation | async-start | bytes 4194304 | tf_op jit(solution)/shard_map/all_to_all | solution.py:15
  19.0 28.6 %all-to-all-done = bf16[8,128,1024]{2,1,0:T(8,128)(2,1)S(1)} async-done(((bf16[8,128,1024]{2,1,0:T(8,128)(2,1)}), bf16[8,128,1024]{2,1,0:T(8,128)(2,1)S(1)}, u32[]{:S(2)}, u32[]{:S(2)}) %all-to-all-start) | async-done | bytes 2097184 | tf_op jit(solution)/shard_map/all_to_all | solution.py:15
  47.6 0.3 convert_reduce_fusion.2
  48.0 0.2 fusion.45
  48.2 0.1 broadcast_in_dim.11
  48.4 35.1 %all_to_all.25 = bf16[16,16,2048]{2,1,0:T(8,128)(2,1)S(1)} all-to-all(bf16[16,16,2048]{2,1,0:T(8,128)(2,1)S(1)} %broadcast_in_dim.11), channel_id=1, replica_groups=mesh['dp'=8,'blk_0'=8,'blk_1'=2,'blk_2'=2] {'blk_0','blk_1'}, dimensions={0} | all-to-all | bytes 2097152 | tf_op jit(solution)/shard_map/all_to_all | solution.py:15
  83.5 0.3 broadcast_in_dim.12
  83.8 7.5 %all_to_all.26 = bf16[2,16,16,2048]{3,2,1,0:T(8,128)(2,1)S(1)} all-to-all(bf16[2,16,16,2048]{3,2,1,0:T(8,128)(2,1)S(1)} %broadcast_in_dim.12), channel_id=1, replica_groups=mesh['dp'=8,'blk_0'=8,'blk_1'=2,'blk_2'=2] {'blk_2'}, dimensions={0} | all-to-all | bytes 4194304 | tf_op jit(solution)/shard_map/all_to_all | solution.py:15
  91.2 0.1 copy.11
  91.4 0.5 fusion.5
  91.8 0.5 fusion.51
  92.3 0.5 fusion.53
  92.8 1.0 copy-done.2
  93.8 0.2 multiply_convert_fusion
  94.0 1.6 broadcast_in_dim.13
  95.6 5.8 %all-to-all-start.3 = ((bf16[8,128,1024]{2,1,0:T(8,128)(2,1)}), bf16[8,128,1024]{2,1,0:T(8,128)(2,1)}, u32[]{:S(2)}, u32[]{:S(2)}) async-start(bf16[8,128,1024]{2,1,0:T(8,128)(2,1)} %broadcast_in_dim.13), calls=%async_computation.3 | async-start | bytes 4194304 | tf_op jit(solution)/shard_map/all_to_all | solution.py:15
  101.4 0.4 fusion.60
  101.8 0.2 fusion.64
  102.0 0.7 fusion.65
  102.7 27.3 %all-to-all-done.3 = bf16[8,128,1024]{2,1,0:T(8,128)(2,1)} async-done(((bf16[8,128,1024]{2,1,0:T(8,128)(2,1)}), bf16[8,128,1024]{2,1,0:T(8,128)(2,1)}, u32[]{:S(2)}, u32[]{:S(2)}) %all-to-all-start.3) | async-done | bytes 2097184 | tf_op jit(solution)/shard_map/all_to_all | solution.py:15
  130.1 2.0 %convert_reduce_fusion.1 = f32[128,1024]{1,0:T(8,128)S(1)} fusion(bf16[8,128,1024]{2,1,0:T(8,128)(2,1)} %all-to-all-done.3), kind=kLoop, calls=%fused_computation.7 | loop fusion | flops 1966080 | bytes 2621440 | tf_op jit(solution)/shard_map/reduce_sum | solution.py:22
  132.1 10.4 %fusion.40 = f32[128,1024]{1,0:T(8,128)S(1)} fusion(bf16[4096,1024]{1,0:T(8,128)(2,1)} %param.4, f32[128,4096]{1,0:T(8,128)} %copy-done, f32[128,1024]{1,0:T(8,128)S(1)} %convert_reduce_fusion.1), kind=kOutput, calls=%fused_computation.42 | convolution fusion | flops 2149711872 | bytes 11534336 | tf_op jit(solution)/shard_map/dot_general | solution.py:144
  142.5 1.8 fusion.15
  144.3 0.3 broadcast_in_dim.14
  144.5 33.3 %all_to_all.27 = bf16[8,128,1024]{2,1,0:T(8,128)(2,1)S(1)} all-to-all(bf16[8,128,1024]{2,1,0:T(8,128)(2,1)S(1)} %broadcast_in_dim.14), channel_id=1, replica_groups=mesh['dp'=8,'blk_0'=8,'blk_1'=2,'blk_2'=2] {'dp'}, dimensions={0} | all-to-all | bytes 4194304 | tf_op jit(solution)/shard_map/all_to_all | solution.py:15
  177.8 0.4 convert_reduce_fusion
  178.2 0.9 multiply_add_fusion
  (14 shorter events, 0.1 us)
Async XLA Ops:
  0.0 8.6 %slice-start = ((s8[8388608]{0:T(1024)(128)(4,1)}), s8[4194304]{0:T(1024)(128)(4,1)S(1)}, s32[]{:S(2)}) async-start(s8[8388608]{0:T(1024)(128)(4,1)} %bitcast.16), calls=%async_computation.5 | async-start | bytes 8388608
  2.1 6.5 %slice-start.1 = ((s8[8388608]{0:T(1024)(128)(4,1)}), s8[4194304]{0:T(1024)(128)(4,1)S(1)}, s32[]{:S(2)}) async-start(s8[8388608]{0:T(1024)(128)(4,1)} %bitcast.16), calls=%async_computation.6 | async-start | bytes 8388608
  8.6 1.4 copy-start
  11.6 36.1 %all-to-all-start = ((bf16[8,128,1024]{2,1,0:T(8,128)(2,1)}), bf16[8,128,1024]{2,1,0:T(8,128)(2,1)S(1)}, u32[]{:S(2)}, u32[]{:S(2)}) async-start(bf16[8,128,1024]{2,1,0:T(8,128)(2,1)} %broadcast_in_dim.10), calls=%async_computation | async-start | bytes 4194304 | tf_op jit(solution)/shard_map/all_to_all | solution.py:15
  19.0 29.0 %copy-start.1 = (f32[128,1024]{1,0:T(8,128)S(1)}, f32[128,1024]{1,0:T(8,128)}, u32[]{:S(2)}) copy-start(f32[128,1024]{1,0:T(8,128)} %param.3) | copy-start | bytes 1572868
  48.2 53.8 %copy-start.3 = (bf16[128,1024]{1,0:T(8,128)(2,1)}, bf16[128,1024]{1,0:T(8,128)(2,1)S(1)}, u32[]{:S(2)}) copy-start(bf16[128,1024]{1,0:T(8,128)(2,1)S(1)} %get-tuple-element.9) | copy-start | bytes 786436
  92.8 1.0 copy-start.2
  95.6 34.5 %all-to-all-start.3 = ((bf16[8,128,1024]{2,1,0:T(8,128)(2,1)}), bf16[8,128,1024]{2,1,0:T(8,128)(2,1)}, u32[]{:S(2)}, u32[]{:S(2)}) async-start(bf16[8,128,1024]{2,1,0:T(8,128)(2,1)} %broadcast_in_dim.13), calls=%async_computation.3 | async-start | bytes 4194304 | tf_op jit(solution)/shard_map/all_to_all | solution.py:15
where the time goes:
time: 179 us
  blocking collectives  75.9 us (42%)
  waiting for transfers between devices  55.9 us (31%)
  matrix products  22.1 us (12%)
  starting transfers between devices  13.3 us (7%)
  other arithmetic  6.55 us (4%)
  local copies, waits for them, and re-layouts  5.14 us (3%)
    all_to_all x3, blocking collectives, from_everyone(): lax.all_to_all(jnp.broadcast_to(value[None], (devices, *value.shape)), ax...  75.9 us
    all_to_all x2, waiting for transfers between devices, from_everyone(): lax.all_to_all(jnp.broadcast_to(value[None], (devices, *value.shape)), ax...  55.9 us
    all_to_all x2, starting transfers between devices, from_everyone(): lax.all_to_all(jnp.broadcast_to(value[None], (devices, *value.shape)), ax...  13.3 us
    dot_general x1, matrix products, shards(): jnp.dot(weighted_rows, data_rows, preferred_element_type=jnp.float32)  10.4 us
    dot_general x1, matrix products, shards(): jnp.einsum('pd,md->pm', x_low, data_rows, preferred_element_type=jnp.floa...  6.47 us
    broadcast_in_dim x5, local copies, waits for them, and re-layouts, from_everyone(): jnp.broadcast_to(value[None], (devices, *value.shape))  3.77 us
  transfers between devices with their start and end apart: 2, of which 2 were waited for; matrix products, arithmetic and copies ran while one was open for 1% of the time, Pallas kernels for 0%

commit v1 on v0

v1 whole, which is shorter than its diff:
```python
import jax
import jax.numpy as jnp
from jax import lax
from jax.experimental import pallas as pl
from jax.experimental.pallas import tpu as pltpu
from jax.sharding import Mesh
from jax.sharding import PartitionSpec as P

DP = ("yh", "x")
BLK = ("z", "yl", "c")
prior_var = 4.0
NCH = 2
F32 = jnp.float32
BF16 = jnp.bfloat16

PEERS = ((1, 2), (1, 1), (1, 3), (0, 2), (1, 0), (0, 1), (0, 3))


def dot_t(a, b):
    return lax.dot_general(a, b, (((1,), (1,)), ((), ())), preferred_element_type=F32)


def dot_n(a, b):
    return lax.dot_general(a, b, (((1,), (0,)), ((), ())), preferred_element_type=F32)


def as_row(col, rows):
    return jnp.broadcast_to(col, (col.shape[0], rows)).T


def make_kernel(feature_count, data_count, particle_count):
    D = feature_count
    inv_band = 1.0 / D
    SR = 16
    NS = 8
    PB = SR * NS
    NZ = 8
    CW = D // NCH
    DCH = 8
    DR = data_count // DCH

    def kernel(
        part_hbm, data_hbm, lab_hbm, out_ref,
        data, part, lab, xl, resid, curv, psb, rbuf, left_s, glow, rx, rs,
        kf, dist, kb, wb, place, own_force, fin,
        load_sem, dps, dpr, bsx, bax, bbx, bcx, bdx, bss, bas, bbs, bcs, bds,
    ):
        yh, x = lax.axis_index("yh"), lax.axis_index("x")
        z, yl, c = lax.axis_index("z"), lax.axis_index("yl"), lax.axis_index("c")
        g = yh * 4 + x
        y = yh * 2 + yl
        ny = lax.rem(y + 1 + 2 * c, 4)
        py = lax.rem(y + 3 + 2 * c, 4)

        def at_dp(dy, dx):
            return lax.rem(yh + dy, 2), lax.rem(x + dx, 4)

        def dev_dp(dy, dx):
            ty, tx = at_dp(dy, dx)
            return {"yh": ty, "x": tx}

        def dev_z(d):
            return {"z": lax.rem(z + d, NZ)}

        def dev_y(t):
            return {"yh": t // 2, "yl": lax.rem(t, 2)}

        dev_core = {"c": 1 - c}
        everyone = (
            [dev_dp(*p) for p in PEERS] + [dev_z(d) for d in range(1, NZ)]
            + [dev_y(ny), dev_y(py), dev_core]
        )
        barrier = pltpu.get_barrier_semaphore()
        for dev in everyone:
            pl.semaphore_signal(barrier, inc=1, device_id=dev, device_id_type=pl.DeviceIdType.MESH)

        load_part = pltpu.make_async_copy(part_hbm, part, load_sem.at[DCH])
        load_lab = pltpu.make_async_copy(lab_hbm, lab, load_sem.at[DCH + 1])
        load_part.start()
        load_lab.start()

        def load_data(i):
            rows = pl.ds(pl.multiple_of(i * DR, DR), DR)
            return pltpu.make_async_copy(data_hbm.at[rows], data.at[rows], load_sem.at[i])

        for i in range(DCH):
            load_data(i).start()

        def remote(src, dst, ssem, rsem, dev):
            return pltpu.make_async_remote_copy(
                src_ref=src, dst_ref=dst, send_sem=ssem, recv_sem=rsem,
                device_id=dev, device_id_type=pl.DeviceIdType.MESH,
            )

        def cols(ch):
            return pl.ds(ch * CW, CW)

        def rs_send(phase, ch):
            for dy, dx in PEERS:
                ty, tx = at_dp(dy, dx)
                remote(
                    psb.at[phase, ty * 4 + tx, :, cols(ch)],
                    rbuf.at[phase, dy * 4 + dx, :, cols(ch)],
                    dps.at[phase, 0, ch], dpr.at[phase, 0, ch], {"yh": ty, "x": tx},
                ).start()

        def seven(phase, kind, ch):
            ref = rbuf.at[phase, pl.ds(1, NS - 1), :, cols(ch)]
            return remote(ref, ref, dps.at[phase, kind, ch], dpr.at[phase, kind, ch], dev_core)

        def rs_total(phase, ch):
            seven(phase, 0, ch).wait_recv()
            total = psb[phase, g, :, cols(ch)].astype(F32)
            for d in range(1, NS):
                total = total + rbuf[phase, d, :, cols(ch)].astype(F32)
            return total

        def ag_send(phase, ref, ch):
            for dy, dx in PEERS:
                remote(
                    ref.at[g, :, cols(ch)], ref.at[g, :, cols(ch)],
                    dps.at[phase, 1, ch], dpr.at[phase, 1, ch], dev_dp(dy, dx),
                ).start()

        def ag_wait(phase, ch):
            seven(phase, 1, ch).wait_recv()

        class Gather:
            def __init__(self, buf, send, a, b, cc, d):
                self.buf, self.send, self.a, self.b, self.c, self.d = buf, send, a, b, cc, d

            def start(self):
                for d in (4, 3, 5, 2, 6, 1, 7):
                    remote(self.buf.at[0], self.buf.at[d], self.send, self.a.at[d], dev_z(d)).start()
                self.pass_on(0)

            def pass_on(self, d):
                remote(self.buf.at[d], self.buf.at[8 + d], self.send, self.b.at[d], dev_y(ny)).start()
                remote(self.buf.at[d], self.buf.at[16 + d], self.send, self.c, dev_core).start()

            def forward_a(self, d):
                remote(self.buf.at[d], self.buf.at[d], self.send, self.a.at[d], dev_core).wait_recv()
                self.pass_on(d)

            def forward_b(self, d):
                remote(self.buf.at[d], self.buf.at[8 + d], self.send, self.b.at[d], dev_core).wait_recv()
                remote(self.buf.at[8 + d], self.buf.at[24 + d], self.send, self.d, dev_core).start()

            def wait_c(self):
                ref = self.buf.at[pl.ds(16, 8)]
                remote(ref, ref, self.send, self.c, dev_core).wait_recv()

            def wait_d(self):
                ref = self.buf.at[pl.ds(24, 8)]
                remote(ref, ref, self.send, self.d, dev_core).wait_recv()

            def drain(self):
                ref = self.buf.at[pl.ds(0, 31)]
                remote(ref, ref, self.send, self.d, dev_core).wait_send()

        ORDER = (1, 7, 2, 6, 3, 5, 4)
        gx = Gather(rx, bsx, bax, bbx, bcx, bdx)
        gs = Gather(rs, bss, bas, bbs, bcs, bds)

        load_part.wait()
        xl[...] = part[...].astype(BF16)
        rx[0] = xl[g]
        load_lab.wait()

        def logits_step(i):
            load_data(i).wait()
            rows = pl.ds(pl.multiple_of(i * DR, DR), DR)
            logits = dot_t(xl[...].reshape(PB, D), data[rows, :])
            p = jax.nn.sigmoid(logits)
            resid[:, rows] = (lab[:, rows].astype(F32) - p).astype(BF16)
            curv[:, rows] = p * (1.0 - p)

        pl.semaphore_wait(barrier, len(everyone))
        gx.start()

        @pl.loop(0, DCH)
        def _(i):
            logits_step(i)

        for ch in range(NCH):
            part_score = dot_n(resid[...], data[:, cols(ch)])
            psb[0, :, :, cols(ch)] = part_score.astype(BF16).reshape(NS, SR, CW)
            rs_send(0, ch)

        for d in ORDER:
            gx.forward_a(d)

        for ch in range(NCH):
            score = rs_total(0, ch) - part[g, :, cols(ch)] / prior_var
            own = score.astype(BF16)
            rs[0, :, cols(ch)] = own
            left_s[g, :, cols(ch)] = own
            ag_send(0, left_s, ch)
        gs.start()

        for d in (0,) + ORDER:
            gx.forward_b(d)
        gx.wait_c()
        gx.wait_d()

        xlow = xl[...].reshape(PB, D)
        xf = xlow.astype(F32)
        left_norm = jnp.sum(xf * xf, axis=1, keepdims=True)
        right_x = rx[...].reshape(32 * SR, D)
        rxf = right_x.astype(F32)
        right_norm = jnp.sum(rxf * rxf, axis=1, keepdims=True)
        distance = left_norm + as_row(right_norm, PB) - 2.0 * dot_t(xlow, right_x)
        kernel_val = jnp.exp(-0.5 * inv_band * distance)
        kf[...] = kernel_val
        dist[...] = distance
        kb[...] = kernel_val.astype(BF16)
        kernel_sum = jnp.sum(kernel_val, axis=1, keepdims=True)

        for d in ORDER:
            gs.forward_a(d)
        for ch in range(NCH):
            ag_wait(0, ch)
        for d in (0,) + ORDER:
            gs.forward_b(d)
        gs.wait_c()
        gs.wait_d()

        slow = left_s[...].reshape(PB, D)
        left_sx = jnp.sum(slow.astype(F32) * xf, axis=1, keepdims=True)
        right_s = rs[...].reshape(32 * SR, D)
        right_sx = jnp.sum(right_s.astype(F32) * rxf, axis=1, keepdims=True)
        gram_ss = dot_t(slow, right_s)
        cross = dot_t(xlow, right_s) + dot_t(slow, right_x)
        bracket = (
            gram_ss + inv_band * (left_sx - cross + as_row(right_sx, PB))
            + D * inv_band - inv_band * inv_band * dist[...]
        )
        weighted = kf[...] * bracket
        wb[...] = weighted.astype(BF16)
        weighted_sum = jnp.sum(weighted, axis=1, keepdims=True)

        for ch in range(NCH):
            rxc = rx[:, :, cols(ch)].reshape(32 * SR, CW)
            rsc = rs[:, :, cols(ch)].reshape(32 * SR, CW)
            kernel_x = dot_n(kb[...], rxc)
            kernel_s = dot_n(kb[...], rsc)
            weighted_x = dot_n(wb[...], rxc)
            xc = xl[:, :, cols(ch)].reshape(PB, CW).astype(F32)
            sc = left_s[:, :, cols(ch)].reshape(PB, CW).astype(F32)
            spread = kernel_sum * xc - kernel_x
            force = (kernel_s + inv_band * spread) / particle_count
            psb[1, :, :, cols(ch)] = force.astype(BF16).reshape(NS, SR, CW)
            rs_send(1, ch)
            place[:, cols(ch)] = (
                -inv_band * (weighted_sum * xc - weighted_x)
                + inv_band * (kernel_sum * sc - kernel_s)
                - 2.0 * inv_band * inv_band * spread
            ) / particle_count

        for ch in range(NCH):
            total = rs_total(1, ch)
            own_force[:, cols(ch)] = total
            glow[g, :, cols(ch)] = total.astype(BF16)
            ag_send(1, glow, ch)
        for ch in range(NCH):
            ag_wait(1, ch)

        @pl.loop(0, DCH)
        def _(i):
            rows = pl.ds(pl.multiple_of(i * DR, DR), DR)
            projected = dot_t(glow[...].reshape(PB, D), data[rows, :])
            resid[:, rows] = (curv[:, rows] * projected).astype(BF16)

        for ch in range(NCH):
            term = dot_n(resid[...], data[:, cols(ch)]) - place[:, cols(ch)]
            psb[2, :, :, cols(ch)] = term.astype(BF16).reshape(NS, SR, CW)
            rs_send(2, ch)

        for ch in range(NCH):
            total = rs_total(2, ch) + own_force[:, cols(ch)] / prior_var
            fin[g, :, cols(ch)] = total.astype(BF16)
            ag_send(2, fin, ch)
        for ch in range(NCH):
            ag_wait(2, ch)
            out_ref[:, cols(ch)] = fin[:, :, cols(ch)].reshape(PB, CW).astype(F32)

        gx.drain()
        gs.drain()
        for phase in range(3):
            for kind in range(2):
                for ch in range(NCH):
                    seven(phase, kind, ch).wait_send()

    V = pltpu.VMEM
    S = pltpu.SemaphoreType.DMA
    scratch = [
        V((data_count, D), BF16), V((NS, SR, D), F32), V((1, data_count), jnp.int32),
        V((NS, SR, D), BF16), V((PB, data_count), BF16), V((PB, data_count), F32),
        V((3, NS, SR, D), BF16), V((3, NS, SR, D), BF16), V((NS, SR, D), BF16), V((NS, SR, D), BF16),
        V((32, SR, D), BF16), V((32, SR, D), BF16),
        V((PB, 32 * SR), F32), V((PB, 32 * SR), F32), V((PB, 32 * SR), BF16), V((PB, 32 * SR), BF16),
        V((PB, D), F32), V((SR, D), F32), V((NS, SR, D), BF16),
        S((DCH + 2,)), S((3, 2, NCH)), S((3, 2, NCH)),
        S, S((NZ,)), S((NZ,)), S, S,
        S, S((NZ,)), S((NZ,)), S, S,
    ]
    return kernel, scratch


def solution(mesh):
    torus = Mesh(mesh.devices.reshape(2, 4, 8, 2, 2), DP + BLK)

    def shards(particles, data_rows, labels):
        rows, feature_count = particles.shape
        kernel, scratch = make_kernel(feature_count, data_rows.shape[0], rows * 32)
        return pl.pallas_call(
            kernel,
            out_shape=jax.ShapeDtypeStruct((rows, feature_count), F32),
            in_specs=[pl.BlockSpec(memory_space=pl.ANY)] * 3,
            out_specs=pl.BlockSpec(memory_space=pltpu.VMEM),
            scratch_shapes=scratch,
            compiler_params=pltpu.CompilerParams(
                collective_id=0, has_side_effects=True, vmem_limit_bytes=60 * 1024 * 1024
            ),
        )(particles.reshape(8, 16, feature_count), data_rows, labels.reshape(1, -1))

    return jax.shard_map(
        shards,
        mesh=torus,
        in_specs=(P(BLK, None), P(DP, None), P(DP)),
        out_specs=P(BLK, None),
        check_vma=False,
    )
```

time: 179 us -> 64.2 us (0.36)
  blocking collectives: 75.9 us -> 0 us
  Pallas kernels: 0 us -> 62.2 us
  waiting for transfers between devices: 55.9 us -> 0 us
  matrix products: 22.1 us -> 0 us
  starting transfers between devices: 13.3 us -> 0 us
  other arithmetic: 6.55 us -> 0 us
  local copies, waits for them, and re-layouts: 5.14 us -> 1.89 us
    all_to_all x3 -> x0, blocking collectives: 75.9 us -> none  [from_everyone(): lax.all_to_all(jnp.broadcast_to(value[None], (devices, *value.shape)), ax...]
    pallas_call x0 -> x1, Pallas kernels: none -> 62.2 us  [shards(): pl.pallas_call(kernel, out_shape=jax.ShapeDtypeStruct((rows, feature_coun...]
    all_to_all x2 -> x0, waiting for transfers between devices: 55.9 us -> none  [from_everyone(): lax.all_to_all(jnp.broadcast_to(value[None], (devices, *value.shape)), ax...]
    dot_general x8 -> x0, matrix products: 22.1 us -> none  [the longest x1 10.4 us: shards(): jnp.dot(weighted_rows, data_rows, preferred_element_type=jnp.float32)]
    all_to_all x2 -> x0, starting transfers between devices: 13.3 us -> none  [from_everyone(): lax.all_to_all(jnp.broadcast_to(value[None], (devices, *value.shape)), ax...]
    broadcast_in_dim x5 -> x0, local copies, waits for them, and re-layouts: 3.77 us -> none  [from_everyone(): jnp.broadcast_to(value[None], (devices, *value.shape))]
    reduce_sum x5 -> x0, other arithmetic: 3.38 us -> none  [the longest x3 2.7 us: over_copies(): return jnp.sum(everything.astype(jnp.float32), axis=0)]
    convert_element_type x3 -> x0, other arithmetic: 2.29 us -> none  [the longest x1 1.22 us: shards(): x_low = particles.astype(jnp.bfloat16)]
  transfers between devices with their start and end apart: 2 -> 0, of which waited for: 2 -> 0; matrix products, arithmetic and copies ran while one was open for 1% -> 0% of each run, Pallas kernels for 0% -> 0%
where the time goes in v1:
time: 64.2 us; the launch traced here: 64.1 us
  Pallas kernels  62.2 us (97%)
  local copies, waits for them, and re-layouts  1.89 us (3%)
    pallas_call x1, Pallas kernels, shards(): pl.pallas_call(kernel, out_shape=jax.ShapeDtypeStruct((rows, feature_coun...  62.2 us
    unnamed x1, local copies, waits for them, and re-layouts  1.89 us

profile of v1, /device:TPU:1, one launch (start us, length us, event | category | flops | bytes accessed | tf_op | source)
XLA Modules:
  0.0 64.1 jit_solution(3709761661662710736)
XLA Ops:
  0.0 62.2 %shard_map.37 = f32[128,1024]{1,0:T(8,128)} custom-call(f32[8,16,1024]{2,1,0:T(8,128)} %bitcast.2, bf16[4096,1024]{1,0:T(8,128)(2,1)} %data_hbm.1, s32[1,4096]{1,0:T(1,128)} %bitcast.3), custom_call_target="tpu_custom_call" | custom-call | tf_op jit(solution)/shard_map/pallas_call | solution.py:316
  62.2 1.9 %copy.5 = f32[128,1024]{1,0:T(8,128)} copy(f32[128,1024]{1,0:T(8,128)} %shard_map.37) | data formatting | bytes 1048576

commit v2 on v1

v2 whole, which is shorter than its diff:
```python
import jax
import jax.numpy as jnp
from jax import lax
from jax.experimental import pallas as pl
from jax.experimental.pallas import tpu as pltpu
from jax.sharding import Mesh
from jax.sharding import PartitionSpec as P

DP = ("yh", "x")
BLK = ("z", "yl", "c")
prior_var = 4.0
NCH = 2
F32 = jnp.float32
BF16 = jnp.bfloat16

PEERS = ((1, 2), (1, 1), (1, 3), (0, 2), (1, 0), (0, 1), (0, 3))


def dot_t(a, b):
    return lax.dot_general(a, b, (((1,), (1,)), ((), ())), preferred_element_type=F32)


def dot_n(a, b):
    return lax.dot_general(a, b, (((1,), (0,)), ((), ())), preferred_element_type=F32)


def as_row(col, rows):
    return jnp.broadcast_to(col, (col.shape[0], rows)).T


def make_kernel(feature_count, data_count, particle_count):
    D = feature_count
    inv_band = 1.0 / D
    SR = 16
    NS = 8
    PB = SR * NS
    NZ = 8
    CW = D // NCH
    DCH = 8
    DR = data_count // DCH

    def kernel(
        part_hbm, data_hbm, lab_hbm, out_ref,
        data, part, lab, xl, resid, curv, psb, rbuf, left_s, glow, rx, rs,
        kf, dist, kb, wb, place, own_force, data_t, lg, acc, ks, spread, ksum,
        load_sem, dps, dpr, bsx, bax, bbx, bcx, bdx, bss, bas, bbs, bcs, bds,
    ):
        yh, x = lax.axis_index("yh"), lax.axis_index("x")
        z, yl, c = lax.axis_index("z"), lax.axis_index("yl"), lax.axis_index("c")
        g = yh * 4 + x
        y = yh * 2 + yl
        ny = lax.rem(y + 1 + 2 * c, 4)
        py = lax.rem(y + 3 + 2 * c, 4)

        def at_dp(dy, dx):
            return lax.rem(yh + dy, 2), lax.rem(x + dx, 4)

        def dev_dp(dy, dx):
            ty, tx = at_dp(dy, dx)
            return {"yh": ty, "x": tx}

        def dev_z(d):
            return {"z": lax.rem(z + d, NZ)}

        def dev_y(t):
            return {"yh": t // 2, "yl": lax.rem(t, 2)}

        dev_core = {"c": 1 - c}
        everyone = (
            [dev_dp(*p) for p in PEERS] + [dev_z(d) for d in range(1, NZ)]
            + [dev_y(ny), dev_y(py), dev_core]
        )
        barrier = pltpu.get_barrier_semaphore()
        for dev in everyone:
            pl.semaphore_signal(barrier, inc=1, device_id=dev, device_id_type=pl.DeviceIdType.MESH)

        load_part = pltpu.make_async_copy(part_hbm, part, load_sem.at[DCH])
        load_lab = pltpu.make_async_copy(lab_hbm, lab, load_sem.at[DCH + 1])
        load_part.start()
        load_lab.start()

        def load_data(i):
            rows = pl.ds(pl.multiple_of(i * DR, DR), DR)
            return pltpu.make_async_copy(data_hbm.at[rows], data.at[rows], load_sem.at[i])

        for i in range(DCH):
            load_data(i).start()

        def remote(src, dst, ssem, rsem, dev):
            return pltpu.make_async_remote_copy(
                src_ref=src, dst_ref=dst, send_sem=ssem, recv_sem=rsem,
                device_id=dev, device_id_type=pl.DeviceIdType.MESH,
            )

        def cols(ch):
            return pl.ds(ch * CW, CW)

        def rs_send(phase, ch):
            for dy, dx in PEERS:
                ty, tx = at_dp(dy, dx)
                remote(
                    psb.at[phase, ty * 4 + tx, :, cols(ch)],
                    rbuf.at[phase, dy * 4 + dx, :, cols(ch)],
                    dps.at[phase, 0, ch], dpr.at[phase, 0, ch], {"yh": ty, "x": tx},
                ).start()

        def seven(phase, kind, ch):
            ref = rbuf.at[phase, pl.ds(1, NS - 1), :, cols(ch)]
            return remote(ref, ref, dps.at[phase, kind, ch], dpr.at[phase, kind, ch], dev_core)

        def rs_total(phase, ch):
            seven(phase, 0, ch).wait_recv()
            total = psb[phase, g, :, cols(ch)].astype(F32)
            for d in range(1, NS):
                total = total + rbuf[phase, d, :, cols(ch)].astype(F32)
            return total

        def ag_send(phase, ref, ch):
            for dy, dx in PEERS:
                remote(
                    ref.at[g, :, cols(ch)], ref.at[g, :, cols(ch)],
                    dps.at[phase, 1, ch], dpr.at[phase, 1, ch], dev_dp(dy, dx),
                ).start()

        def ag_wait(phase, ch):
            seven(phase, 1, ch).wait_recv()

        ORDER = (4, 3, 5, 2, 6, 1, 7)

        class Gather:
            def __init__(self, buf, send, a, b, cc, d):
                self.buf, self.send, self.a, self.b, self.c, self.d = buf, send, a, b, cc, d

            def start(self):
                for d in ORDER:
                    remote(self.buf.at[0], self.buf.at[d], self.send, self.a.at[d], dev_z(d)).start()
                self.pass_on(0)

            def pass_on(self, d):
                remote(self.buf.at[d], self.buf.at[16 + d], self.send, self.b.at[d], dev_y(ny)).start()
                remote(self.buf.at[d], self.buf.at[8 + d], self.send, self.c, dev_core).start()

            def forward_a(self, d):
                remote(self.buf.at[d], self.buf.at[d], self.send, self.a.at[d], dev_core).wait_recv()
                self.pass_on(d)

            def forward_b(self, d):
                remote(self.buf.at[d], self.buf.at[16 + d], self.send, self.b.at[d], dev_core).wait_recv()
                remote(self.buf.at[16 + d], self.buf.at[24 + d], self.send, self.d, dev_core).start()

            def wait_c(self):
                ref = self.buf.at[pl.ds(8, 8)]
                remote(ref, ref, self.send, self.c, dev_core).wait_recv()

            def wait_d(self):
                ref = self.buf.at[pl.ds(24, 8)]
                remote(ref, ref, self.send, self.d, dev_core).wait_recv()

            def drain(self):
                ref = self.buf.at[pl.ds(0, 31)]
                remote(ref, ref, self.send, self.d, dev_core).wait_send()

        gx = Gather(rx, bsx, bax, bbx, bcx, bdx)
        gs = Gather(rs, bss, bas, bbs, bcs, bds)

        with jax.named_scope("load_x"):
            load_part.wait()
            xl[...] = part[...].astype(BF16)
            rx[0] = xl[g]
            load_lab.wait()

        with jax.named_scope("barrier"):
            pl.semaphore_wait(barrier, len(everyone))
            gx.start()

        def rows_of(i):
            return pl.ds(i * DR, DR)

        def turn(i):
            load_data(i).wait()
            data_t[:, rows_of(i)] = data[rows_of(i), :].T

        def logits(i):
            lg[i % 2] = dot_n(xl[...].reshape(PB, D), data_t[:, rows_of(i)])

        def squash(i):
            p = jax.nn.sigmoid(lg[i % 2])
            resid[:, rows_of(i)] = (lab[:, rows_of(i)].astype(F32) - p).astype(BF16)
            curv[:, rows_of(i)] = p * (1.0 - p)

        def collect(i):
            term = dot_n(resid[:, rows_of(i)], data[rows_of(i), :])
            if i == 0:
                acc[...] = term
            elif i < DCH - 1:
                acc[...] += term
            else:
                psb[0] = (acc[...] + term).astype(BF16).reshape(NS, SR, D)

        with jax.named_scope("score"):
            stages = (turn, logits, squash, collect)
            for step in range(DCH + len(stages) - 1):
                for k, stage in enumerate(stages):
                    if 0 <= step - k < DCH:
                        stage(step - k)
            for ch in range(NCH):
                rs_send(0, ch)

        with jax.named_scope("fwd_a_x"):
            for d in ORDER:
                gx.forward_a(d)

        with jax.named_scope("rs0"):
            for ch in range(NCH):
                score = rs_total(0, ch) - part[g, :, cols(ch)] / prior_var
                own = score.astype(BF16)
                rs[0, :, cols(ch)] = own
                left_s[g, :, cols(ch)] = own
            gs.start()
            for ch in range(NCH):
                ag_send(0, left_s, ch)

        with jax.named_scope("fwd_b_x"):
            for d in (0,) + ORDER:
                gx.forward_b(d)
            gx.wait_c()
            gx.wait_d()

        with jax.named_scope("pair_x"):
            xlow = xl[...].reshape(PB, D)
            xf = xlow.astype(F32)
            left_norm = jnp.sum(xf * xf, axis=1, keepdims=True)
            right_x = rx[...].reshape(32 * SR, D)
            rxf = right_x.astype(F32)
            right_norm = jnp.sum(rxf * rxf, axis=1, keepdims=True)
            distance = left_norm + as_row(right_norm, PB) - 2.0 * dot_t(xlow, right_x)
            kernel_val = jnp.exp(-0.5 * inv_band * distance)
            kf[...] = kernel_val
            dist[...] = distance
            kb[...] = kernel_val.astype(BF16)
            kernel_sum = jnp.sum(kernel_val, axis=1, keepdims=True)
            ksum[...] = kernel_sum
            spread[...] = kernel_sum * xf - dot_n(kb[...], right_x)

        with jax.named_scope("fwd_a_s"):
            for d in ORDER:
                gs.forward_a(d)
            gs.wait_c()
        with jax.named_scope("fwd_b_s"):
            for d in (0,) + ORDER:
                gs.forward_b(d)
            gs.wait_d()

        with jax.named_scope("force"):
            for ch in range(NCH):
                kernel_s = dot_n(kb[...], rs[:, :, cols(ch)].reshape(32 * SR, CW))
                ks[:, cols(ch)] = kernel_s
                force = (kernel_s + inv_band * spread[:, cols(ch)]) / particle_count
                psb[1, :, :, cols(ch)] = force.astype(BF16).reshape(NS, SR, CW)
                rs_send(1, ch)

        with jax.named_scope("place"):
            for ch in range(NCH):
                ag_wait(0, ch)
            slow = left_s[...].reshape(PB, D)
            xlow = xl[...].reshape(PB, D)
            xf = xlow.astype(F32)
            sf = slow.astype(F32)
            left_sx = jnp.sum(sf * xf, axis=1, keepdims=True)
            right_x = rx[...].reshape(32 * SR, D)
            right_s = rs[...].reshape(32 * SR, D)
            right_sx = jnp.sum(right_s.astype(F32) * right_x.astype(F32), axis=1, keepdims=True)
            cross = dot_t(xlow, right_s) + dot_t(slow, right_x)
            bracket = (
                dot_t(slow, right_s) + inv_band * (left_sx - cross + as_row(right_sx, PB))
                + D * inv_band - inv_band * inv_band * dist[...]
            )
            weighted = kf[...] * bracket
            wb[...] = weighted.astype(BF16)
            weighted_sum = jnp.sum(weighted, axis=1, keepdims=True)
            weighted_x = dot_n(wb[...], right_x)
            place[...] = (
                -inv_band * (weighted_sum * xf - weighted_x)
                + inv_band * (ksum[...] * sf - ks[...])
                - 2.0 * inv_band * inv_band * spread[...]
            ) / particle_count

        with jax.named_scope("rs1"):
            for ch in range(NCH):
                total = rs_total(1, ch)
                own_force[:, cols(ch)] = total
                glow[g, :, cols(ch)] = total.astype(BF16)
                ag_send(1, glow, ch)
        with jax.named_scope("ag1"):
            for ch in range(NCH):
                ag_wait(1, ch)

        with jax.named_scope("proj"):
            for i in range(DCH):
                projected = dot_n(glow[...].reshape(PB, D), data_t[:, rows_of(i)])
                resid[:, rows_of(i)] = (curv[:, rows_of(i)] * projected).astype(BF16)

        with jax.named_scope("term"):
            for ch in range(NCH):
                term = dot_n(resid[...], data[:, cols(ch)]) - place[:, cols(ch)]
                psb[2, :, :, cols(ch)] = term.astype(BF16).reshape(NS, SR, CW)
                rs_send(2, ch)

        with jax.named_scope("rs2"):
            for ch in range(NCH):
                total = rs_total(2, ch) + own_force[:, cols(ch)] / prior_var
                out_ref[g, :, cols(ch)] = total.astype(BF16)
                ag_send(2, out_ref, ch)
        with jax.named_scope("ag2"):
            for ch in range(NCH):
                ag_wait(2, ch)

        gx.drain()
        gs.drain()
        for phase in range(3):
            for kind in range(2):
                for ch in range(NCH):
                    seven(phase, kind, ch).wait_send()

    V = pltpu.VMEM
    S = pltpu.SemaphoreType.DMA
    scratch = [
        V((data_count, D), BF16), V((NS, SR, D), F32), V((1, data_count), jnp.int32),
        V((NS, SR, D), BF16), V((PB, data_count), BF16), V((PB, data_count), F32),
        V((3, NS, SR, D), BF16), V((3, NS, SR, D), BF16), V((NS, SR, D), BF16), V((NS, SR, D), BF16),
        V((32, SR, D), BF16), V((32, SR, D), BF16),
        V((PB, 32 * SR), F32), V((PB, 32 * SR), F32), V((PB, 32 * SR), BF16), V((PB, 32 * SR), BF16),
        V((PB, D), F32), V((SR, D), F32),
        V((D, data_count), BF16), V((2, PB, DR), F32), V((PB, D), F32), V((PB, D), F32), V((PB, D), F32),
        V((PB, 1), F32),
        S((DCH + 2,)), S((3, 2, NCH)), S((3, 2, NCH)),
        S, S((NZ,)), S((NZ,)), S, S,
        S, S((NZ,)), S((NZ,)), S, S,
    ]
    return kernel, scratch


def solution(mesh):
    torus = Mesh(mesh.devices.reshape(2, 4, 8, 2, 2), DP + BLK)

    def shards(particles, data_rows, labels):
        rows, feature_count = particles.shape
        kernel, scratch = make_kernel(feature_count, data_rows.shape[0], rows * 32)
        descent = pl.pallas_call(
            kernel,
            out_shape=jax.ShapeDtypeStruct((8, 16, feature_count), BF16),
            in_specs=[pl.BlockSpec(memory_space=pl.ANY)] * 3,
            out_specs=pl.BlockSpec(memory_space=pltpu.VMEM),
            scratch_shapes=scratch,
            compiler_params=pltpu.CompilerParams(
                collective_id=0, has_side_effects=True, vmem_limit_bytes=44 * 1024 * 1024
            ),
        )(*[pltpu.with_memory_space_constraint(v, pltpu.HBM) for v in (particles.reshape(8, 16, feature_count), data_rows, labels.reshape(1, -1))])
        return descent.reshape(rows, feature_count).astype(F32)

    return jax.shard_map(
        shards,
        mesh=torus,
        in_specs=(P(BLK, None), P(DP, None), P(DP)),
        out_specs=P(BLK, None),
        check_vma=False,
    )
```

time: 64.2 us -> 56.3 us (0.88)
  Pallas kernels: 62.2 us -> 55.4 us
  local copies, waits for them, and re-layouts: 1.89 us -> 0 us
  other arithmetic: 0 us -> 0.86 us
    pallas_call x1, Pallas kernels: 62.2 us -> 55.4 us  [shards(): pl.pallas_call(kernel, out_shape=jax.ShapeDtypeStruct((8, 16, feature_cou...]
    unnamed x1 -> x0, local copies, waits for them, and re-layouts: 1.89 us -> none
    convert_element_type x0 -> x1, other arithmetic: none -> 0.86 us  [shards(): return descent.reshape(rows, feature_count).astype(F32)]
where the time goes in v2:
time: 56.3 us; the launch traced here: 56.2 us
  Pallas kernels  55.4 us (98%)
  other arithmetic  0.86 us (2%)
    pallas_call x1, Pallas kernels, shards(): pl.pallas_call(kernel, out_shape=jax.ShapeDtypeStruct((8, 16, feature_cou...  55.4 us

profile of v2, /device:TPU:1, one launch (start us, length us, event | category | flops | bytes accessed | tf_op | source)
XLA Modules:
  0.0 56.2 jit_solution(14358590245168861530)
XLA Ops:
  0.0 55.4 %shard_map.37 = bf16[8,16,1024]{2,1,0:T(8,128)(2,1)S(1)} custom-call(f32[8,16,1024]{2,1,0:T(8,128)} %bitcast.5, bf16[4096,1024]{1,0:T(8,128)(2,1)} %data_hbm.1, s32[1,4096]{1,0:T(1,128)} %bitcast.6), custom_call_target="tpu_custom_call" | custom-call | tf_op jit(solution)/shard_map/pallas_call | solution.py:349
  55.4 0.9 %bitcast_convert_fusion = f32[128,1024]{1,0:T(8,128)} fusion(bf16[8,16,1024]{2,1,0:T(8,128)(2,1)S(1)} %shard_map.37), kind=kLoop, calls=%fused_computation | loop fusion | flops 131072 | bytes 786432 | tf_op jit(solution)/shard_map/convert_element_type | solution.py:359

commit v3 on v2

v3 whole, which is shorter than its diff:
```python
import jax
import jax.numpy as jnp
from jax import lax
from jax.experimental import pallas as pl
from jax.experimental.pallas import tpu as pltpu
from jax.sharding import Mesh
from jax.sharding import PartitionSpec as P

DP = ("yh", "x")
BLK = ("z", "yl", "c")
prior_var = 4.0
NCH = 2
F32 = jnp.float32
BF16 = jnp.bfloat16

PEERS = ((1, 2), (1, 1), (1, 3), (0, 2), (1, 0), (0, 1), (0, 3))

OTHERS = ((0, 2), (1, 2), (0, 1), (1, 1), (0, 3), (1, 3), (1, 0), (0, 0))
FORCE_TO = (
    (1, 1, 2), (0, 0, 2), (0, 1, 2), (1, 1, 1), (1, 1, 3), (0, 0, 1), (0, 1, 1), (0, 0, 3),
    (0, 1, 3), (1, 0, 2), (1, 1, 0), (0, 1, 0), (0, 0, 0), (1, 0, 1), (1, 0, 3),
)
ORDER = (4, 3, 5, 2, 6, 1, 7)
FIRST = 3


def dot_t(a, b):
    return lax.dot_general(a, b, (((1,), (1,)), ((), ())), preferred_element_type=F32)


def dot_n(a, b):
    return lax.dot_general(a, b, (((1,), (0,)), ((), ())), preferred_element_type=F32)


def as_row(col, rows):
    return jnp.broadcast_to(col, (col.shape[0], rows)).T


def make_kernel(feature_count, data_count, particle_count):
    D = feature_count
    inv_band = 1.0 / D
    SR = 16
    NS = 8
    PB = SR * NS
    NZ = 8
    NR = 2 * NZ * SR
    CW = D // NCH
    DCH = 8
    DR = data_count // DCH

    def kernel(
        part_hbm, data_hbm, lab_hbm, out_ref,
        data, part, lab, lx, ls, resid, curv, psb, psf, psp, rbuf, rforce, rplace, glow, rx, rs,
        kf, dist, kb, wb, place, own_force, data_t, lg, acc, ks, spread, ksum,
        load_sem, sent, rsr, agr, gxr, gsr, nbr,
    ):
        yh, x = lax.axis_index("yh"), lax.axis_index("x")
        z, yl, c = lax.axis_index("z"), lax.axis_index("yl"), lax.axis_index("c")
        g = yh * 4 + x
        y = yh * 2 + yl

        def at_dp(dy, dx):
            return lax.rem(yh + dy, 2), lax.rem(x + dx, 4)

        def dev_dp(dy, dx):
            ty, tx = at_dp(dy, dx)
            return {"yh": ty, "x": tx}

        def dev_other(dy, dx):
            return {**dev_dp(dy, dx), "yl": 1 - yl}

        def dev_z(d):
            return {"z": lax.rem(z + d, NZ)}

        def dev_y(t):
            return {"yh": t // 2, "yl": lax.rem(t, 2)}

        y_up, y_down = dev_y(lax.rem(y + 1, 4)), dev_y(lax.rem(y + 3, 4))
        dev_core = {"c": 1 - c}
        everyone = (
            [dev_dp(*p) for p in PEERS] + [dev_other(*p) for p in OTHERS]
            + [dev_z(d) for d in range(1, NZ)] + [dev_core]
        )
        barrier = pltpu.get_barrier_semaphore()
        for dev in everyone:
            pl.semaphore_signal(barrier, inc=1, device_id=dev, device_id_type=pl.DeviceIdType.MESH)

        load_part = pltpu.make_async_copy(part_hbm, part, load_sem.at[DCH])
        load_lab = pltpu.make_async_copy(lab_hbm, lab, load_sem.at[DCH + 1])
        load_part.start()
        load_lab.start()

        def rows_of(i):
            return pl.ds(i * DR, DR)

        def load_data(i):
            return pltpu.make_async_copy(data_hbm.at[rows_of(i)], data.at[rows_of(i)], load_sem.at[i])

        for i in range(DCH):
            load_data(i).start()

        def remote(src, dst, ssem, rsem, dev):
            return pltpu.make_async_remote_copy(
                src_ref=src, dst_ref=dst, send_sem=ssem, recv_sem=rsem,
                device_id=dev, device_id_type=pl.DeviceIdType.MESH,
            )

        def cols(ch):
            return pl.ds(ch * CW, CW)

        def wait_bytes(shares, rsem, width):
            ref = rforce.at[pl.ds(0, shares), :, width]
            remote(ref, ref, sent.at[0], rsem, dev_core).wait_recv()

        def rs_send(k, src, dst, ch):
            for dy, dx in PEERS:
                ty, tx = at_dp(dy, dx)
                remote(
                    src.at[ty * 4 + tx, :, cols(ch)], dst.at[dy * 4 + dx, :, cols(ch)],
                    sent.at[k], rsr.at[k, ch], {"yh": ty, "x": tx},
                ).start()

        def rs_total(k, src, buf, ch, sources):
            wait_bytes(sources - 1, rsr.at[k, ch], cols(ch))
            total = src[g, :, cols(ch)].astype(F32)
            for d in range(1, sources):
                total = total + buf[d, :, cols(ch)].astype(F32)
            return total

        def ag_send(k, ref, ch):
            for dy, dx in PEERS:
                remote(
                    ref.at[g, :, cols(ch)], ref.at[g, :, cols(ch)],
                    sent.at[3 + k], agr.at[k, ch], dev_dp(dy, dx),
                ).start()

        class Gather:
            def __init__(self, buf, send, recv):
                self.buf, self.send, self.recv = buf, send, recv

            def start(self):
                for p, d in enumerate(ORDER):
                    remote(
                        self.buf.at[0], self.buf.at[1 + p], self.send,
                        self.recv.at[0 if p < FIRST else 1], dev_z(d),
                    ).start()
                self.pass_on(0, 1)

            def pass_on(self, at, n):
                remote(
                    self.buf.at[pl.ds(at, n)], self.buf.at[pl.ds(8 + at, n)], self.send, self.recv.at[2], dev_core
                ).start()

            def forward(self, group):
                at, n = (1, FIRST) if group == 0 else (1 + FIRST, 7 - FIRST)
                ref = self.buf.at[pl.ds(at, n)]
                remote(ref, ref, self.send, self.recv.at[group], dev_core).wait_recv()
                self.pass_on(at, n)

            def wait(self):
                ref = self.buf.at[pl.ds(8, 8)]
                remote(ref, ref, self.send, self.recv.at[2], dev_core).wait_recv()

        gx = Gather(rx, sent.at[6], gxr)
        gs = Gather(rs, sent.at[7], gsr)

        with jax.named_scope("load_x"):
            load_part.wait()
            lx[pl.ds(0, NS)] = part[...].astype(BF16)
            rx[0] = lx[g]
            load_lab.wait()

        with jax.named_scope("barrier"):
            pl.semaphore_wait(barrier, len(everyone))
            gx.start()
            remote(lx.at[pl.ds(0, 4)], lx.at[pl.ds(8, 4)], sent.at[8], nbr.at[0], y_up).start()
            remote(lx.at[pl.ds(4, 4)], lx.at[pl.ds(12, 4)], sent.at[8], nbr.at[0], y_down).start()

        def turn(i):
            load_data(i).wait()
            data_t[:, rows_of(i)] = data[rows_of(i), :].T

        def logits(i):
            lg[i % 2] = dot_n(lx[pl.ds(0, NS)].reshape(PB, D), data_t[:, rows_of(i)])

        def squash(i):
            p = jax.nn.sigmoid(lg[i % 2])
            resid[:, rows_of(i)] = (lab[:, rows_of(i)].astype(F32) - p).astype(BF16)
            curv[:, rows_of(i)] = p * (1.0 - p)

        def collect(i):
            term = dot_n(resid[:, rows_of(i)], data[rows_of(i), :])
            if i == 0:
                acc[...] = term
            elif i < DCH - 1:
                acc[...] += term
            else:
                psb[0] = (acc[...] + term).astype(BF16).reshape(NS, SR, D)

        with jax.named_scope("score"):
            stages = (turn, logits, squash, collect)
            for step in range(DCH + len(stages) - 1):
                for k, stage in enumerate(stages):
                    if 0 <= step - k < DCH:
                        stage(step - k)
            for ch in range(NCH):
                rs_send(0, psb.at[0], rbuf.at[0], ch)

        with jax.named_scope("fwd_x"):
            gx.forward(0)
            gx.forward(1)

        with jax.named_scope("rs0"):
            for ch in range(NCH):
                score = rs_total(0, psb.at[0], rbuf.at[0], ch, NS) - part[g, :, cols(ch)] / prior_var
                own = score.astype(BF16)
                rs[0, :, cols(ch)] = own
                ls[g, :, cols(ch)] = own
            gs.start()
            for dy, dx in PEERS:
                remote(ls.at[g], ls.at[g], sent.at[3], agr.at[0, 0], dev_dp(dy, dx)).start()
            for dy, dx in OTHERS:
                remote(rs.at[0], ls.at[8 + g], sent.at[3], agr.at[0, 0], dev_other(dy, dx)).start()

        with jax.named_scope("pair_x"):
            wait_bytes(8, nbr.at[0], slice(None))
            gx.wait()
            xlow = lx[...].reshape(2 * PB, D)
            xf = xlow.astype(F32)
            left_norm = jnp.sum(xf * xf, axis=1, keepdims=True)
            right_x = rx[...].reshape(NR, D)
            rxf = right_x.astype(F32)
            right_norm = jnp.sum(rxf * rxf, axis=1, keepdims=True)
            distance = left_norm + as_row(right_norm, 2 * PB) - 2.0 * dot_t(xlow, right_x)
            kernel_val = jnp.exp(-0.5 * inv_band * distance)
            kf[...] = kernel_val
            dist[...] = distance
            kb[...] = kernel_val.astype(BF16)
            kernel_sum = jnp.sum(kernel_val, axis=1, keepdims=True)
            ksum[...] = kernel_sum
            spread[...] = kernel_sum * xf - dot_n(kb[...], right_x)

        with jax.named_scope("fwd_s"):
            gs.forward(0)
            gs.forward(1)
        with jax.named_scope("wait_s"):
            gs.wait()

        with jax.named_scope("force"):
            for ch in range(NCH):
                kernel_s = dot_n(kb[...], rs[:, :, cols(ch)].reshape(NR, CW))
                ks[:, cols(ch)] = kernel_s
                force = (kernel_s + inv_band * spread[:, cols(ch)]) / particle_count
                psf[:, :, cols(ch)] = force.astype(BF16).reshape(2 * NS, SR, CW)
                for own, dy, dx in FORCE_TO:
                    ty, tx = at_dp(dy, dx)
                    at = 0 if own else NS
                    remote(
                        psf.at[at + ty * 4 + tx, :, cols(ch)], rforce.at[at + dy * 4 + dx, :, cols(ch)],
                        sent.at[1], rsr.at[1, ch], {"yh": ty, "x": tx, "yl": yl if own else 1 - yl},
                    ).start()

        with jax.named_scope("place"):
            wait_bytes(15, agr.at[0, 0], slice(None))
            slow = ls[...].reshape(2 * PB, D)
            xlow = lx[...].reshape(2 * PB, D)
            xf = xlow.astype(F32)
            sf = slow.astype(F32)
            left_sx = jnp.sum(sf * xf, axis=1, keepdims=True)
            right_x = rx[...].reshape(NR, D)
            right_s = rs[...].reshape(NR, D)
            right_sx = jnp.sum(right_s.astype(F32) * right_x.astype(F32), axis=1, keepdims=True)
            cross = dot_t(xlow, right_s) + dot_t(slow, right_x)
            bracket = (
                dot_t(slow, right_s) + inv_band * (left_sx - cross + as_row(right_sx, 2 * PB))
                + D * inv_band - inv_band * inv_band * dist[...]
            )
            weighted = kf[...] * bracket
            wb[...] = weighted.astype(BF16)
            weighted_sum = jnp.sum(weighted, axis=1, keepdims=True)
            weighted_x = dot_n(wb[...], right_x)
            moved = (
                -inv_band * (weighted_sum * xf - weighted_x)
                + inv_band * (ksum[...] * sf - ks[...])
                - 2.0 * inv_band * inv_band * spread[...]
            ) / particle_count
            place[...] = moved[:PB]
            psp[...] = moved[PB:].astype(BF16).reshape(NS, SR, D)

        with jax.named_scope("rs1"):
            for ch in range(NCH):
                total = rs_total(1, psf, rforce, ch, 2 * NS)
                own_force[:, cols(ch)] = total
                glow[g, :, cols(ch)] = total.astype(BF16)
                ag_send(1, glow, ch)
            for dy, dx in OTHERS:
                ty, tx = at_dp(dy, dx)
                remote(
                    psp.at[ty * 4 + tx], rplace.at[dy * 4 + dx], sent.at[9], nbr.at[1],
                    {"yh": ty, "x": tx, "yl": 1 - yl},
                ).start()
        with jax.named_scope("ag1"):
            for ch in range(NCH):
                wait_bytes(NS - 1, agr.at[1, ch], cols(ch))

        with jax.named_scope("proj"):
            for i in range(DCH):
                projected = dot_n(glow[...].reshape(PB, D), data_t[:, rows_of(i)])
                resid[:, rows_of(i)] = (curv[:, rows_of(i)] * projected).astype(BF16)

        with jax.named_scope("term"):
            for ch in range(NCH):
                term = dot_n(resid[...], data[:, cols(ch)]) - place[:, cols(ch)]
                psb[1, :, :, cols(ch)] = term.astype(BF16).reshape(NS, SR, CW)
                rs_send(2, psb.at[1], rbuf.at[1], ch)

        with jax.named_scope("base"):
            wait_bytes(NS, nbr.at[1], slice(None))
            base = own_force[...] / prior_var
            for d in range(NS):
                base = base - rplace[d].astype(F32)
            own_force[...] = base

        with jax.named_scope("rs2"):
            for ch in range(NCH):
                total = rs_total(2, psb.at[1], rbuf.at[1], ch, NS) + own_force[:, cols(ch)]
                out_ref[g, :, cols(ch)] = total.astype(BF16)
                ag_send(2, out_ref, ch)
        with jax.named_scope("ag2"):
            for ch in range(NCH):
                wait_bytes(NS - 1, agr.at[2, ch], cols(ch))

        with jax.named_scope("drain"):
            for k, shares in enumerate((7, 15, 7, 15, 7, 7, 15, 15, 8, 8)):
                ref = rforce.at[pl.ds(0, shares)]
                remote(ref, ref, sent.at[k], nbr.at[0], dev_core).wait_send()

    V = pltpu.VMEM
    S = pltpu.SemaphoreType.DMA
    scratch = [
        V((data_count, D), BF16), V((NS, SR, D), F32), V((1, data_count), jnp.int32),
        V((2 * NS, SR, D), BF16), V((2 * NS, SR, D), BF16), V((PB, data_count), BF16), V((PB, data_count), F32),
        V((2, NS, SR, D), BF16), V((2 * NS, SR, D), BF16), V((NS, SR, D), BF16),
        V((2, NS, SR, D), BF16), V((2 * NS, SR, D), BF16), V((NS, SR, D), BF16), V((NS, SR, D), BF16),
        V((2 * NZ, SR, D), BF16), V((2 * NZ, SR, D), BF16),
        V((2 * PB, NR), F32), V((2 * PB, NR), F32), V((2 * PB, NR), BF16), V((2 * PB, NR), BF16),
        V((PB, D), F32), V((SR, D), F32),
        V((D, data_count), BF16), V((2, PB, DR), F32), V((PB, D), F32), V((2 * PB, D), F32), V((2 * PB, D), F32),
        V((2 * PB, 1), F32),
        S((DCH + 2,)), S((10,)), S((3, NCH)), S((3, NCH)), S((3,)), S((3,)), S((2,)),
    ]
    return kernel, scratch


def solution(mesh):
    torus = Mesh(mesh.devices.reshape(2, 4, 8, 2, 2), DP + BLK)

    def shards(particles, data_rows, labels):
        rows, feature_count = particles.shape
        kernel, scratch = make_kernel(feature_count, data_rows.shape[0], rows * 32)
        descent = pl.pallas_call(
            kernel,
            out_shape=jax.ShapeDtypeStruct((8, 16, feature_count), BF16),
            in_specs=[pl.BlockSpec(memory_space=pl.ANY)] * 3,
            out_specs=pl.BlockSpec(memory_space=pltpu.VMEM),
            scratch_shapes=scratch,
            compiler_params=pltpu.CompilerParams(
                collective_id=0, has_side_effects=True, vmem_limit_bytes=44 * 1024 * 1024
            ),
        )(*[pltpu.with_memory_space_constraint(v, pltpu.HBM) for v in (particles.reshape(8, 16, feature_count), data_rows, labels.reshape(1, -1))])
        return descent.reshape(rows, feature_count).astype(F32)

    return jax.shard_map(
        shards,
        mesh=torus,
        in_specs=(P(BLK, None), P(DP, None), P(DP)),
        out_specs=P(BLK, None),
        check_vma=False,
    )
```

time: 56.3 us -> 54.7 us (0.972)
  Pallas kernels: 55.4 us -> 53.8 us
    pallas_call x1, Pallas kernels: 55.4 us -> 53.8 us  [shards(): pl.pallas_call(kernel, out_shape=jax.ShapeDtypeStruct((8, 16, feature_cou...]
where the time goes in v3:
time: 54.7 us; the launch traced here: 54.6 us
  Pallas kernels  53.8 us (98%)
  other arithmetic  0.86 us (2%)
    pallas_call x1, Pallas kernels, shards(): pl.pallas_call(kernel, out_shape=jax.ShapeDtypeStruct((8, 16, feature_cou...  53.8 us

profile of v3, /device:TPU:1, one launch (start us, length us, event | category | flops | bytes accessed | tf_op | source)
XLA Modules:
  0.0 54.6 jit_solution(12608682327853444391)
XLA Ops:
  0.0 53.8 %shard_map.37 = bf16[8,16,1024]{2,1,0:T(8,128)(2,1)S(1)} custom-call(f32[8,16,1024]{2,1,0:T(8,128)} %bitcast.5, bf16[4096,1024]{1,0:T(8,128)(2,1)} %data_hbm.1, s32[1,4096]{1,0:T(1,128)} %bitcast.6), custom_call_target="tpu_custom_call" | custom-call | tf_op jit(solution)/shard_map/pallas_call | solution.py:361
  53.8 0.9 %bitcast_convert_fusion = f32[128,1024]{1,0:T(8,128)} fusion(bf16[8,16,1024]{2,1,0:T(8,128)(2,1)S(1)} %shard_map.37), kind=kLoop, calls=%fused_computation | loop fusion | flops 131072 | bytes 786432 | tf_op jit(solution)/shard_map/convert_element_type | solution.py:371

commit v4 on v3

--- a/solution.py
+++ b/solution.py
@@ -170,14 +170,10 @@
             rx[0] = lx[g]
             load_lab.wait()
 
-        with jax.named_scope("barrier"):
-            pl.semaphore_wait(barrier, len(everyone))
-            gx.start()
-            remote(lx.at[pl.ds(0, 4)], lx.at[pl.ds(8, 4)], sent.at[8], nbr.at[0], y_up).start()
-            remote(lx.at[pl.ds(4, 4)], lx.at[pl.ds(12, 4)], sent.at[8], nbr.at[0], y_down).start()
-
         def turn(i):
-            load_data(i).wait()
+            if i % 2 == 0:
+                load_data(i).wait()
+                load_data(i + 1).wait()
             data_t[:, rows_of(i)] = data[rows_of(i), :].T
 
         def logits(i):
@@ -200,15 +196,17 @@
         with jax.named_scope("score"):
             stages = (turn, logits, squash, collect)
             for step in range(DCH + len(stages) - 1):
+                if step == 2:
+                    with jax.named_scope("barrier"):
+                        pl.semaphore_wait(barrier, len(everyone))
+                        gx.start()
+                        remote(lx.at[pl.ds(0, 4)], lx.at[pl.ds(8, 4)], sent.at[8], nbr.at[0], y_up).start()
+                        remote(lx.at[pl.ds(4, 4)], lx.at[pl.ds(12, 4)], sent.at[8], nbr.at[0], y_down).start()
                 for k, stage in enumerate(stages):
                     if 0 <= step - k < DCH:
                         stage(step - k)
             for ch in range(NCH):
                 rs_send(0, psb.at[0], rbuf.at[0], ch)
-
-        with jax.named_scope("fwd_x"):
-            gx.forward(0)
-            gx.forward(1)
 
         with jax.named_scope("rs0"):
             for ch in range(NCH):
@@ -221,6 +219,10 @@
                 remote(ls.at[g], ls.at[g], sent.at[3], agr.at[0, 0], dev_dp(dy, dx)).start()
             for dy, dx in OTHERS:
                 remote(rs.at[0], ls.at[8 + g], sent.at[3], agr.at[0, 0], dev_other(dy, dx)).start()
+
+        with jax.named_scope("fwd_x"):
+            gx.forward(0)
+            gx.forward(1)
 
         with jax.named_scope("pair_x"):
             wait_bytes(8, nbr.at[0], slice(None))
@@ -293,12 +295,8 @@
                 own_force[:, cols(ch)] = total
                 glow[g, :, cols(ch)] = total.astype(BF16)
                 ag_send(1, glow, ch)
-            for dy, dx in OTHERS:
-                ty, tx = at_dp(dy, dx)
-                remote(
-                    psp.at[ty * 4 + tx], rplace.at[dy * 4 + dx], sent.at[9], nbr.at[1],
-                    {"yh": ty, "x": tx, "yl": 1 - yl},
-                ).start()
+            remote(psp.at[pl.ds(0, 4)], rplace.at[pl.ds(0, 4)], sent.at[9], nbr.at[1], y_up).start()
+            remote(psp.at[pl.ds(4, 4)], rplace.at[pl.ds(4, 4)], sent.at[9], nbr.at[1], y_down).start()
         with jax.named_scope("ag1"):
             for ch in range(NCH):
                 wait_bytes(NS - 1, agr.at[1, ch], cols(ch))
@@ -311,19 +309,17 @@
         with jax.named_scope("term"):
             for ch in range(NCH):
                 term = dot_n(resid[...], data[:, cols(ch)]) - place[:, cols(ch)]
+                if ch == 0:
+                    acc[:, cols(ch)] = term
+                    wait_bytes(NS, nbr.at[1], slice(None))
+                    term = acc[:, cols(ch)]
+                term = term - rplace[:, :, cols(ch)].reshape(PB, CW).astype(F32)
                 psb[1, :, :, cols(ch)] = term.astype(BF16).reshape(NS, SR, CW)
                 rs_send(2, psb.at[1], rbuf.at[1], ch)
 
-        with jax.named_scope("base"):
-            wait_bytes(NS, nbr.at[1], slice(None))
-            base = own_force[...] / prior_var
-            for d in range(NS):
-                base = base - rplace[d].astype(F32)
-            own_force[...] = base
-
         with jax.named_scope("rs2"):
             for ch in range(NCH):
-                total = rs_total(2, psb.at[1], rbuf.at[1], ch, NS) + own_force[:, cols(ch)]
+                total = rs_total(2, psb.at[1], rbuf.at[1], ch, NS) + own_force[:, cols(ch)] / prior_var
                 out_ref[g, :, cols(ch)] = total.astype(BF16)
                 ag_send(2, out_ref, ch)
         with jax.named_scope("ag2"):

time: 54.7 us -> 53 us (0.969)
  Pallas kernels: 53.8 us -> 52.1 us
    pallas_call x1, Pallas kernels: 53.8 us -> 52.1 us  [shards(): pl.pallas_call(kernel, out_shape=jax.ShapeDtypeStruct((8, 16, feature_cou...]
where the time goes in v4:
time: 53 us; the launch traced here: 52.9 us
  Pallas kernels  52.1 us (98%)
  other arithmetic  0.86 us (2%)
    pallas_call x1, Pallas kernels, shards(): pl.pallas_call(kernel, out_shape=jax.ShapeDtypeStruct((8, 16, feature_cou...  52.1 us

profile of v4, /device:TPU:1, one launch (start us, length us, event | category | flops | bytes accessed | tf_op | source)
XLA Modules:
  0.0 52.9 jit_solution(16818961411483975905)
XLA Ops:
  0.0 52.1 %shard_map.37 = bf16[8,16,1024]{2,1,0:T(8,128)(2,1)S(1)} custom-call(f32[8,16,1024]{2,1,0:T(8,128)} %bitcast.5, bf16[4096,1024]{1,0:T(8,128)(2,1)} %data_hbm.1, s32[1,4096]{1,0:T(1,128)} %bitcast.6), custom_call_target="tpu_custom_call" | custom-call | tf_op jit(solution)/shard_map/pallas_call | solution.py:357
  52.1 0.9 %bitcast_convert_fusion = f32[128,1024]{1,0:T(8,128)} fusion(bf16[8,16,1024]{2,1,0:T(8,128)(2,1)S(1)} %shard_map.37), kind=kLoop, calls=%fused_computation | loop fusion | flops 131072 | bytes 786432 | tf_op jit(solution)/shard_map/convert_element_type | solution.py:367

commit v5 on v4

--- a/solution.py
+++ b/solution.py
@@ -45,7 +45,8 @@
     NZ = 8
     NR = 2 * NZ * SR
     CW = D // NCH
-    DCH = 8
+    DCH = 16
+    GROUPS = ((0, 4), (4, 4), (8, 4), (12, 2), (14, 2))
     DR = data_count // DCH
 
     def kernel(
@@ -85,8 +86,8 @@
         for dev in everyone:
             pl.semaphore_signal(barrier, inc=1, device_id=dev, device_id_type=pl.DeviceIdType.MESH)
 
-        load_part = pltpu.make_async_copy(part_hbm, part, load_sem.at[DCH])
-        load_lab = pltpu.make_async_copy(lab_hbm, lab, load_sem.at[DCH + 1])
+        load_part = pltpu.make_async_copy(part_hbm, part, load_sem.at[len(GROUPS)])
+        load_lab = pltpu.make_async_copy(lab_hbm, lab, load_sem.at[len(GROUPS) + 1])
         load_part.start()
         load_lab.start()
 
@@ -94,9 +95,10 @@
             return pl.ds(i * DR, DR)
 
         def load_data(i):
-            return pltpu.make_async_copy(data_hbm.at[rows_of(i)], data.at[rows_of(i)], load_sem.at[i])
-
-        for i in range(DCH):
+            rows = pl.ds(GROUPS[i][0] * DR, GROUPS[i][1] * DR)
+            return pltpu.make_async_copy(data_hbm.at[rows], data.at[rows], load_sem.at[i])
+
+        for i in range(len(GROUPS)):
             load_data(i).start()
 
         def remote(src, dst, ssem, rsem, dev):
@@ -138,13 +140,13 @@
             def __init__(self, buf, send, recv):
                 self.buf, self.send, self.recv = buf, send, recv
 
-            def start(self):
+            def start(self, at=slice(None)):
                 for p, d in enumerate(ORDER):
                     remote(
-                        self.buf.at[0], self.buf.at[1 + p], self.send,
+                        self.buf.at[0, :, at], self.buf.at[1 + p, :, at], self.send,
                         self.recv.at[0 if p < FIRST else 1], dev_z(d),
                     ).start()
-                self.pass_on(0, 1)
+                remote(self.buf.at[0, :, at], self.buf.at[8, :, at], self.send, self.recv.at[2], dev_core).start()
 
             def pass_on(self, at, n):
                 remote(
@@ -171,9 +173,9 @@
             load_lab.wait()
 
         def turn(i):
-            if i % 2 == 0:
-                load_data(i).wait()
-                load_data(i + 1).wait()
+            for k, (first, _) in enumerate(GROUPS):
+                if i == first:
+                    load_data(k).wait()
             data_t[:, rows_of(i)] = data[rows_of(i), :].T
 
         def logits(i):
@@ -196,7 +198,7 @@
         with jax.named_scope("score"):
             stages = (turn, logits, squash, collect)
             for step in range(DCH + len(stages) - 1):
-                if step == 2:
+                if step == 4:
                     with jax.named_scope("barrier"):
                         pl.semaphore_wait(barrier, len(everyone))
                         gx.start()
@@ -214,7 +216,7 @@
                 own = score.astype(BF16)
                 rs[0, :, cols(ch)] = own
                 ls[g, :, cols(ch)] = own
-            gs.start()
+                gs.start(cols(ch))
             for dy, dx in PEERS:
                 remote(ls.at[g], ls.at[g], sent.at[3], agr.at[0, 0], dev_dp(dy, dx)).start()
             for dy, dx in OTHERS:
@@ -302,9 +304,10 @@
                 wait_bytes(NS - 1, agr.at[1, ch], cols(ch))
 
         with jax.named_scope("proj"):
-            for i in range(DCH):
-                projected = dot_n(glow[...].reshape(PB, D), data_t[:, rows_of(i)])
-                resid[:, rows_of(i)] = (curv[:, rows_of(i)] * projected).astype(BF16)
+            for i in range(8):
+                rows = pl.ds(i * (data_count // 8), data_count // 8)
+                projected = dot_n(glow[...].reshape(PB, D), data_t[:, rows])
+                resid[:, rows] = (curv[:, rows] * projected).astype(BF16)
 
         with jax.named_scope("term"):
             for ch in range(NCH):
@@ -343,7 +346,7 @@
         V((PB, D), F32), V((SR, D), F32),
         V((D, data_count), BF16), V((2, PB, DR), F32), V((PB, D), F32), V((2 * PB, D), F32), V((2 * PB, D), F32),
         V((2 * PB, 1), F32),
-        S((DCH + 2,)), S((10,)), S((3, NCH)), S((3, NCH)), S((3,)), S((3,)), S((2,)),
+        S((len(GROUPS) + 2,)), S((10,)), S((3, NCH)), S((3, NCH)), S((3,)), S((3,)), S((2,)),
     ]
     return kernel, scratch
 

time: 53 us -> 52.6 us (level)
  no operation moved by 1% of the time
where the time goes in v5:
time: 52.6 us; the launch traced here: 52.5 us
  Pallas kernels  51.7 us (98%)
  other arithmetic  0.86 us (2%)
    pallas_call x1, Pallas kernels, shards(): pl.pallas_call(kernel, out_shape=jax.ShapeDtypeStruct((8, 16, feature_cou...  51.7 us

profile of v5, /device:TPU:1, one launch (start us, length us, event | category | flops | bytes accessed | tf_op | source)
XLA Modules:
  0.0 52.5 jit_solution(9125363182028532956)
XLA Ops:
  0.0 51.7 %shard_map.37 = bf16[8,16,1024]{2,1,0:T(8,128)(2,1)S(1)} custom-call(f32[8,16,1024]{2,1,0:T(8,128)} %bitcast.5, bf16[4096,1024]{1,0:T(8,128)(2,1)} %data_hbm.1, s32[1,4096]{1,0:T(1,128)} %bitcast.6), custom_call_target="tpu_custom_call" | custom-call | tf_op jit(solution)/shard_map/pallas_call | solution.py:360
  51.7 0.9 %bitcast_convert_fusion = f32[128,1024]{1,0:T(8,128)} fusion(bf16[8,16,1024]{2,1,0:T(8,128)(2,1)S(1)} %shard_map.37), kind=kLoop, calls=%fused_computation | loop fusion | flops 131072 | bytes 786432 | tf_op jit(solution)/shard_map/convert_element_type | solution.py:370

commit v6 on v5

--- a/solution.py
+++ b/solution.py
@@ -198,7 +198,7 @@
         with jax.named_scope("score"):
             stages = (turn, logits, squash, collect)
             for step in range(DCH + len(stages) - 1):
-                if step == 4:
+                if step == 7:
                     with jax.named_scope("barrier"):
                         pl.semaphore_wait(barrier, len(everyone))
                         gx.start()

time: 52.6 us -> 52.2 us (level)
  no operation moved by 1% of the time
where the time goes in v6:
time: 52.2 us; the launch traced here: 52.1 us
  Pallas kernels  51.3 us (98%)
  other arithmetic  0.86 us (2%)
    pallas_call x1, Pallas kernels, shards(): pl.pallas_call(kernel, out_shape=jax.ShapeDtypeStruct((8, 16, feature_cou...  51.3 us

profile of v6, /device:TPU:1, one launch (start us, length us, event | category | flops | bytes accessed | tf_op | source)
XLA Modules:
  0.0 52.1 jit_solution(10512451725360544934)
XLA Ops:
  0.0 51.3 %shard_map.37 = bf16[8,16,1024]{2,1,0:T(8,128)(2,1)S(1)} custom-call(f32[8,16,1024]{2,1,0:T(8,128)} %bitcast.5, bf16[4096,1024]{1,0:T(8,128)(2,1)} %data_hbm.1, s32[1,4096]{1,0:T(1,128)} %bitcast.6), custom_call_target="tpu_custom_call" | custom-call | tf_op jit(solution)/shard_map/pallas_call | solution.py:360
  51.3 0.9 %bitcast_convert_fusion = f32[128,1024]{1,0:T(8,128)} fusion(bf16[8,16,1024]{2,1,0:T(8,128)(2,1)S(1)} %shard_map.37), kind=kLoop, calls=%fused_computation | loop fusion | flops 131072 | bytes 786432 | tf_op jit(solution)/shard_map/convert_element_type | solution.py:370

commit v7 on v6

--- a/solution.py
+++ b/solution.py
@@ -17,8 +17,8 @@
 
 OTHERS = ((0, 2), (1, 2), (0, 1), (1, 1), (0, 3), (1, 3), (1, 0), (0, 0))
 FORCE_TO = (
-    (1, 1, 2), (0, 0, 2), (0, 1, 2), (1, 1, 1), (1, 1, 3), (0, 0, 1), (0, 1, 1), (0, 0, 3),
-    (0, 1, 3), (1, 0, 2), (1, 1, 0), (0, 1, 0), (0, 0, 0), (1, 0, 1), (1, 0, 3),
+    (1, 1, 2), (0, 1, 2), (0, 0, 2), (1, 0, 2), (1, 1, 1), (1, 1, 3), (0, 1, 1), (0, 1, 3),
+    (0, 0, 1), (0, 0, 3), (1, 0, 1), (1, 0, 3), (1, 1, 0), (0, 1, 0), (0, 0, 0),
 )
 ORDER = (4, 3, 5, 2, 6, 1, 7)
 FIRST = 3

time: 52.2 us -> 52.7 us (level)
  no operation moved by 1% of the time
where the time goes in v7:
time: 52.7 us
  Pallas kernels  51.8 us (98%)
  other arithmetic  0.86 us (2%)
    pallas_call x1, Pallas kernels, shards(): pl.pallas_call(kernel, out_shape=jax.ShapeDtypeStruct((8, 16, feature_cou...  51.8 us

profile of v7, /device:TPU:1, one launch (start us, length us, event | category | flops | bytes accessed | tf_op | source)
XLA Modules:
  0.0 52.7 jit_solution(6746396631667066481)
XLA Ops:
  0.0 51.8 %shard_map.37 = bf16[8,16,1024]{2,1,0:T(8,128)(2,1)S(1)} custom-call(f32[8,16,1024]{2,1,0:T(8,128)} %bitcast.5, bf16[4096,1024]{1,0:T(8,128)(2,1)} %data_hbm.1, s32[1,4096]{1,0:T(1,128)} %bitcast.6), custom_call_target="tpu_custom_call" | custom-call | tf_op jit(solution)/shard_map/pallas_call | solution.py:360
  51.8 0.9 %bitcast_convert_fusion = f32[128,1024]{1,0:T(8,128)} fusion(bf16[8,16,1024]{2,1,0:T(8,128)(2,1)S(1)} %shard_map.37), kind=kLoop, calls=%fused_computation | loop fusion | flops 131072 | bytes 786432 | tf_op jit(solution)/shard_map/convert_element_type | solution.py:370
